TPU v7x, 32 devices: a whole 2x2x4 slice. The times are simulated.
32 devices in a mesh: layer: 8 (over y, x, core), tensor: 4 (over z).
Axes of the slice: x: 2, y: 2, z: 4, core: 2. Of those that a mesh axis runs over, the one named last changes fastest.
Arguments:
- gradient: bfloat16 [8, 1024, 8192], P(None, 'tensor', 'layer'), may hold values from -8 to 8
- row_basis: bfloat16 [8, 1024, 256], P('layer', 'tensor'), may hold values from -0.1875 to 0.1875
- column_basis: bfloat16 [8, 8192, 256], P('layer', 'tensor'), may hold values from -0.0625 to 0.0625
- row_eigen: float32 [8, 256], P('layer'), may hold values from 0.01 to 10
- column_eigen: float32 [8, 256], P('layer'), may hold values from 0.01 to 10
- row_escape: float32 [8], P('layer'), may hold values from 0.02 to 0.2
- column_escape: float32 [8], P('layer'), may hold values from 0.02 to 0.2
Outputs:
- update: bfloat16 [8, 1024, 8192], P(None, 'tensor', 'layer')
All inputs are finite; a program needn't handle non-finite values.
Results may differ from a plain program's by a relative error of at most 0.0055.
Values may be sent and summed in bfloat16 or wider, within the bound.
A program may use at most 128 MiB of HBM per device.

v0:
```python
import jax
import jax.numpy as jnp
from jax import lax
from jax.sharding import PartitionSpec as P


def coefficients(row_eigen, column_eigen, row_escape, column_escape):
    row_base = row_escape ** (-0.25)
    column_base = column_escape ** (-0.25)
    row_coef = (row_eigen + row_escape[:, None]) ** (-0.25) - row_base[:, None]
    column_coef = (column_eigen + column_escape[:, None]) ** (-0.25) - column_base[:, None]
    return (row_base, column_base, row_coef, column_coef)


def group_norm(local_block):
    partial_sq = jnp.sum(jnp.square(local_block.astype(jnp.float32)), axis=(1, 2))
    return lax.psum(partial_sq, "tensor")


def finish(raw_update, grad_sq):
    update_sq = lax.psum(jnp.sum(jnp.square(raw_update), axis=(1, 2)), "tensor")
    factor = jnp.sqrt((grad_sq + 1.0) / (update_sq + 1.0))
    return (raw_update * factor[:, None, None]).astype(jnp.bfloat16)


def body(gradient, row_basis, column_basis, row_eigen, column_eigen, row_escape, column_escape):
    row_base, column_base, row_coef, column_coef = coefficients(
        row_eigen, column_eigen, row_escape, column_escape
    )
    both_base = (row_base * column_base)[:, None, None]
    group_block = lax.all_to_all(gradient, "layer", split_axis=0, concat_axis=2, tiled=True)
    grad_sq = group_norm(group_block)
    own_proj = lax.psum_scatter(
        jnp.einsum(
            "lrk,lrd->dlk", row_basis, group_block, preferred_element_type=jnp.float32
        ).astype(jnp.bfloat16),
        "tensor",
        scatter_dimension=0,
        tiled=True,
    ).astype(jnp.float32)
    scaled = (own_proj * row_coef[None]).astype(jnp.bfloat16)
    core_part = jnp.einsum("dlk,ldj->lkj", scaled, column_basis, preferred_element_type=jnp.float32)
    core_mat = lax.psum(core_part.astype(jnp.bfloat16), "tensor")
    whole_columns = lax.all_gather(column_basis, "tensor", axis=1, tiled=True)
    middle = jnp.einsum(
        "lrd,ldk->lrk", group_block, whole_columns, preferred_element_type=jnp.float32
    )
    row_term = jnp.einsum(
        "lrk,dlk->lrd",
        row_basis,
        lax.all_gather(scaled, "tensor", axis=0, tiled=True),
        preferred_element_type=jnp.float32,
    )
    mixed = row_base[:, None, None] * middle + jnp.einsum(
        "lrk,lkj->lrj", row_basis, core_mat, preferred_element_type=jnp.float32
    )
    left_factor = (mixed * column_coef[:, None, :]).astype(jnp.bfloat16)
    raw_update = both_base * group_block.astype(jnp.float32) + column_base[:, None, None] * row_term
    raw_update = raw_update + jnp.einsum(
        "lrk,ldk->lrd", left_factor, whole_columns, preferred_element_type=jnp.float32
    )
    rows_block = finish(raw_update, grad_sq)
    return lax.all_to_all(rows_block, "layer", split_axis=2, concat_axis=0, tiled=True)


def solution(mesh):
    in_specs = (
        P(None, "tensor", "layer"),
        P("layer", "tensor", None),
        P("layer", "tensor", None),
        P("layer", None),
        P("layer", None),
        P("layer"),
        P("layer"),
    )
    out_specs = P(None, "tensor", "layer")
    return jax.shard_map(body, mesh=mesh, in_specs=in_specs, out_specs=out_specs, check_vma=False)
```

profile of v0, /device:TPU:0, one launch (start us, length us, event | category | flops | bytes accessed | tf_op | source)
XLA Modules:
  0.0 558.4 jit_solution(9425964493506922182)
XLA Ops:
  6.5 0.0 copy-start
  6.5 0.0 reduce-scatter.2.cloned.1.call-start
  6.5 54.5 %all_to_all.36 = bf16[8,256,1024]{2,1,0:T(8,128)(2,1)} all-to-all(bf16[8,256,1024]{2,1,0:T(8,128)(2,1)} %param.7), channel_id=1, replica_groups=mesh['layer'=8,'tensor'=4] {'layer'}, dimensions={0} | all-to-all | bytes 8388608 | tf_op jit(solution)/shard_map/all_to_all | solution.py:31
  61.0 6.4 %copy.15 = bf16[1,256,8,1024]{1,3,2,0:T(8,128)(2,1)} copy(bf16[1,256,8,1024]{3,1,2,0:T(8,128)(2,1)} %bitcast.80) | data formatting | bytes 8388608 | tf_op jit(solution)/shard_map/all_to_all | solution.py:31
  67.4 0.0 copy-done
  67.4 5.4 fusion.2
  72.8 0.0 copy-start.4
  72.8 0.0 copy-start.5
  72.8 0.0 reduce-scatter.2.cloned.1.call-update
  72.9 0.0 all-gather.5.cloned.1.call-start
  72.9 0.7 all-gather.5.cloned.1.call-update
  73.6 0.0 all-gather.3.cloned.1.call-start
  74.4 0.0 copy-done.4
  74.4 75.4 %reduce-scatter.2.cloned.1.call-done = bf16[2048,1,256]{2,0,1:T(8,128)(2,1)} async-done(((bf16[8192,1,256]{2,0,1:T(8,128)(2,1)}), bf16[2048,1,256]{2,0,1:T(8,128)(2,1)}) %reduce-scatter.2.cloned.1.call-update) | async-done | bytes 1048592 | tf_op jit(solution)/shard_map/reduce_scatter | solution.py:33
  149.8 2.4 multiply_convert_fusion.1
  152.2 0.0 all-gather.3.cloned.1.call-update
  152.3 0.0 all-reduce.3.cloned.1.call-start
  153.0 0.0 copy-done.5
  153.0 4.9 multiply_reduce_fusion.1
  157.9 0.0 copy-start.2
  158.0 0.0 copy-start.3
  158.0 74.7 %all-gather.5.cloned.1.call-done = bf16[1,8192,256]{2,1,0:T(8,128)(2,1)} async-done(((bf16[1,2048,256]{2,1,0:T(8,128)(2,1)}), bf16[1,8192,256]{2,1,0:T(8,128)(2,1)}) %all-gather.5.cloned.1.call-update) | async-done | bytes 4194320 | tf_op jit(solution)/shard_map/all_gather | solution.py:44
  232.7 4.8 fusion.10
  237.4 0.0 copy-done.2
  237.4 0.0 copy-done.3
  237.5 1.1 convolution_convert_fusion.1
  238.6 0.0 all-reduce.3.cloned.1.call-update
  238.6 75.0 %all-gather.3.cloned.1.call-done = bf16[8192,1,256]{2,0,1:T(8,128)(2,1)} async-done(((bf16[2048,1,256]{2,0,1:T(8,128)(2,1)}), bf16[8192,1,256]{2,0,1:T(8,128)(2,1)}) %all-gather.3.cloned.1.call-update) | async-done | bytes 4194320 | tf_op jit(solution)/shard_map/all_gather | solution.py:51
  313.6 8.0 %fusion.1 = f32[256,8192]{0,1:T(8,128)} fusion(bf16[256,8192]{0,1:T(8,128)(2,1)} %bitcast.79, bf16[8192,1,256]{2,0,1:T(8,128)(2,1)} %all-gather.3.cloned.1.call-done, f32[]{:T(128)} %bitcast.4, f32[]{:T(128)} %bitcast, bf16[1,256,256]{2,1,0:T(8,128)(2,1)S(1)} %copy-done), kind=kOutput, calls=%fused_computation.3 | convolution fusion | flops 1082130432 | bytes 16908296 | tf_op jit(solution)/shard_map/lrk,dlk->lrd/dot_general | solution.py:48
  321.6 27.3 %all-reduce.3.cloned.1.call-done = bf16[256,256]{1,0:T(8,128)(2,1)} async-done(((bf16[256,256]{1,0:T(8,128)(2,1)}), bf16[256,256]{1,0:T(8,128)(2,1)}) %all-reduce.3.cloned.1.call-update) | async-done | bytes 131088 | tf_op jit(solution)/shard_map/psum | solution.py:43
  348.9 11.0 %multiply_reduce_fusion = (f32[]{:T(128)}, f32[256,8192]{0,1:T(8,128)}) fusion(f32[256,8192]{0,1:T(8,128)} %fusion.1, bf16[1,8192,256]{2,1,0:T(8,128)(2,1)} %all-gather.5.cloned.1.call-done, f32[256,256]{1,0:T(8,128)S(1)} %fusion.10, bf16[256,256]{1,0:T(8,128)(2,1)} %all-reduce.3.cloned.1.call-done, bf16[1,256,256]{2,1,0:T(8,128)(2,1)S(1)} %copy-done, ...), kind=kOutput, calls=%fused_computation.7 | convolution fusion | flops 1113784320 | bytes 21496836 | tf_op jit(solution)/shard_map/lrk,ldk->lrd/dot_general | solution.py:59
  359.9 11.3 %all-reduce = (f32[1]{0:T(128)}, f32[1]{0:T(128)}) all-reduce(f32[1]{0:T(128)} %bitcast.19, f32[1]{0:T(128)} %bitcast.20), channel_id=1, replica_groups=mesh['layer'=8,'tensor'=4] {'tensor'}, use_global_device_ids=true, to_apply=%region_3.0 | all-reduce | flops 2 | bytes 16 | tf_op jit(solution)/shard_map/psum | solution.py:17
  372.5 4.1 fusion.3
  376.5 49.5 %copy.24 = bf16[1,256,8192]{1,0,2:T(2,128)(2,1)} copy(bf16[1,256,8192]{1,2,0:T(8,128)(2,1)S(1)} %fusion.3) | data formatting | bytes 8388608 | tf_op jit(solution)/shard_map/convert_element_type | solution.py:23
  426.1 0.5 broadcast.23
  426.6 43.5 %reduce.4 = bf16[8192,256]{1,0:T(8,128)(2,1)} reduce(bf16[8192,1,256]{2,1,0:T(2,128)(2,1)} %bitcast.81, bf16[]{:T(256)} %broadcast.23), dimensions={1}, to_apply=%bitcast.74.reduce_sub_computation | reduce | bytes 8388610
  470.1 7.0 %reshape.90 = bf16[8,2,131072]{2,1,0:T(2,128)(2,1)} reshape(bf16[8192,256]{1,0:T(8,128)(2,1)} %reduce.4) | data formatting | bytes 8388608
  477.1 53.6 %all_to_all.37 = bf16[8,2,131072]{2,1,0:T(2,128)(2,1)} all-to-all(bf16[8,2,131072]{2,1,0:T(2,128)(2,1)} %reshape.90), channel_id=1, replica_groups=mesh['layer'=8,'tensor'=4] {'layer'}, dimensions={0} | all-to-all | bytes 8388608 | tf_op jit(solution)/shard_map/all_to_all | solution.py:63
  530.6 8.7 %reshape.91 = bf16[8192,1,256]{2,1,0:T(2,128)(2,1)} reshape(bf16[8,2,131072]{2,1,0:T(2,128)(2,1)} %all_to_all.37) | data formatting | bytes 8388608
  539.4 6.1 %copy.22 = bf16[1,256,8192]{1,2,0:T(8,128)(2,1)} copy(bf16[1,256,8192]{1,0,2:T(2,128)(2,1)} %bitcast.82) | data formatting | bytes 8388608
  545.4 0.0 copy-start.1
  545.4 6.5 %copy.19 = bf16[8,256,1024]{2,1,0:T(8,128)(2,1)} copy(bf16[8,256,1024]{1,2,0:T(8,128)(2,1)} %bitcast.83) | data formatting | bytes 8388608 | tf_op jit(solution)/shard_map/all_to_all | solution.py:63
  551.9 0.0 copy-done.1
  (2 shorter events, 0.0 us)
Async XLA Ops:
  6.5 60.9 %copy-start = (bf16[1,256,256]{2,1,0:T(8,128)(2,1)S(1)}, bf16[1,256,256]{2,1,0:T(8,128)(2,1)}, u32[]{:S(2)}) copy-start(bf16[1,256,256]{2,1,0:T(8,128)(2,1)} %param.8) | copy-start | bytes 393220
  6.5 143.3 %reduce-scatter.2.cloned.1.call-start = ((), (), s32[]{:S(2)}) async-start(), calls=%async_computation.3 | async-start | bytes 5242880 | tf_op jit(solution)/shard_map/reduce_scatter | solution.py:33
  72.8 1.5 copy-start.4
  72.8 80.2 %copy-start.5 = (f32[1,256]{1,0:T(1,128)S(1)}, f32[1,256]{1,0:T(1,128)}, u32[]{:S(2)}) copy-start(f32[1,256]{1,0:T(1,128)} %param.11) | copy-start | bytes 3076
  72.9 159.8 %all-gather.5.cloned.1.call-start = ((), (), s32[]{:S(2)}) async-start(), calls=%async_computation.5 | async-start | bytes 5242880 | tf_op jit(solution)/shard_map/all_gather | solution.py:44
  73.6 239.9 %all-gather.3.cloned.1.call-start = ((), (), s32[]{:S(2)}) async-start(), calls=%async_computation.4 | async-start | bytes 5242880 | tf_op jit(solution)/shard_map/all_gather | solution.py:51
  152.3 196.6 %all-reduce.3.cloned.1.call-start = ((), (), s32[]{:S(2)}) async-start(), calls=%async_computation.6 | async-start | bytes 262144 | tf_op jit(solution)/shard_map/psum | solution.py:43
  157.9 79.5 %copy-start.2 = (bf16[2048,1,256]{2,0,1:T(8,128)(2,1)S(1)}, bf16[2048,1,256]{2,0,1:T(8,128)(2,1)}, u32[]{:S(2)}) copy-start(bf16[2048,1,256]{2,0,1:T(8,128)(2,1)} %multiply_convert_fusion.1) | copy-start | bytes 3145732
  158.0 79.5 %copy-start.3 = (bf16[1,2048,256]{2,1,0:T(8,128)(2,1)S(1)}, bf16[1,2048,256]{2,1,0:T(8,128)(2,1)}, u32[]{:S(2)}) copy-start(bf16[1,2048,256]{2,1,0:T(8,128)(2,1)} %param.9) | copy-start | bytes 3145732
  545.4 6.5 %copy-start.1 = (bf16[1,256,256]{2,1,0:T(8,128)(2,1)S(1)}, bf16[1,256,256]{2,1,0:T(8,128)(2,1)}, u32[]{:S(2)}) copy-start(bf16[1,256,256]{2,1,0:T(8,128)(2,1)} %param.8) | copy-start | bytes 393220
Sparse Core Ops, SparseCore 0:
  73.0 76.7 reduce-scatter.1
  151.4 81.2 all-gather.4
  234.3 79.2 all-gather.2
  315.7 33.1 all-reduce.2
where the time goes:
time: 559 us; the launch traced here: 558 us
  waiting for transfers between devices  253 us (45%)
  blocking collectives  119 us (21%)
  local copies, waits for them, and re-layouts  84.7 us (15%)
  other arithmetic  54.9 us (10%)
  matrix products  30.3 us (5%)
  between operations  15.9 us (3%)
    reduce_scatter x1, waiting for transfers between devices, body(): lax.psum_scatter(jnp.einsum('lrk,lrd->dlk', row_basis, group_block, prefe...  75.4 us
    all_gather x1, waiting for transfers between devices, body(): lax.all_gather(scaled, 'tensor', axis=0, tiled=True)  75 us
    all_gather x1, waiting for transfers between devices, body(): whole_columns = lax.all_gather(column_basis, 'tensor', axis=1, tiled=True)  74.7 us
    all_to_all x1, blocking collectives, body(): lax.all_to_all(gradient, 'layer', split_axis=0, concat_axis=2, tiled=True)  54.5 us
    all_to_all x1, blocking collectives, body(): lax.all_to_all(rows_block, 'layer', split_axis=2, concat_axis=0, tiled=True)  53.6 us
    convert_element_type x1, local copies, waits for them, and re-layouts, finish(): return (raw_update * factor[:, None, None]).astype(jnp.bfloat16)  49.5 us
    unnamed x1, other arithmetic  43.5 us
    psum x1, waiting for transfers between devices, body(): core_mat = lax.psum(core_part.astype(jnp.bfloat16), 'tensor')  27.3 us
  transfers between devices with their start and end apart: 4, of which 4 were waited for; matrix products, arithmetic and copies ran while one was open for 4% of the time, Pallas kernels for 0%

commit v1 on v0

v1 whole, which is shorter than its diff:
```python
import functools

import jax
import jax.numpy as jnp
from jax import lax
from jax.experimental import pallas as pl
from jax.experimental.pallas import tpu as pltpu
from jax.sharding import PartitionSpec as P

MESH = pl.DeviceIdType.MESH
F32 = jnp.float32
BF16 = jnp.bfloat16


def remote(src, dst, send, recv, axis, index):
    return pltpu.make_async_remote_copy(
        src_ref=src,
        dst_ref=dst,
        send_sem=send,
        recv_sem=recv,
        device_id={axis: index},
        device_id_type=MESH,
    )


def loop(lo, hi, fn):
    def step(i, carry):
        fn(i)
        return carry

    lax.fori_loop(lo, hi, step, 0)


def dot(a, b):
    return jnp.dot(a, b, preferred_element_type=F32)


def kernel(
    L, T,
    g, rows_basis, rows_basis_t, cols, dr, dc, base,
    out,
    gg, own, pin, qin, pout, qout, call, mid, left, core_out, core_in, raw_out, raw_in,
    gacc, uacc, nsend, nrecv, fsend, frecv,
    gs, gr, cs, cr, ps, pr, qs, qr, ks, kr, os_, or_, ns, nr, fs, fr,
):
    me = lax.axis_index("layer")
    t = lax.axis_index("tensor")
    W = g.shape[2]
    Cr = cols.shape[0]
    right, lft = t + 1, t - 1
    has_right, has_left = t < T - 1, t > 0

    barrier = pltpu.get_barrier_semaphore()
    loop(1, L, lambda d: pl.semaphore_signal(
        barrier, inc=1, device_id={"layer": lax.rem(me + d, L)}, device_id_type=MESH))
    loop(1, T, lambda d: pl.semaphore_signal(
        barrier, inc=1, device_id={"tensor": lax.rem(t + d, T)}, device_id_type=MESH))
    pl.semaphore_wait(barrier, L + T - 2)

    def g_copy(slot, dst):
        return remote(g.at[dst], gg.at[slot], gs.at[dst], gr.at[slot], "layer", dst)

    def c_rows(s):
        return call.at[pl.ds(pl.multiple_of(s * Cr, Cr), Cr)]

    def c_copy(src, s, h, side):
        return remote(src, c_rows(s), cs.at[side, h], cr.at[s], "tensor", right if side == 0 else lft)

    pl.when(has_right)(lambda: c_copy(cols, t, 0, 0).start())
    pl.when(has_left)(lambda: c_copy(cols, t, 0, 1).start())
    loop(1, L, lambda d: g_copy(me, lax.rem(me + d, L)).start())
    gg[me] = g[me]
    call[pl.ds(pl.multiple_of(t * Cr, Cr), Cr), :] = cols[...]
    gacc[...] = jnp.zeros_like(gacc)
    uacc[...] = jnp.zeros_like(uacc)
    mid[...] = jnp.zeros_like(mid)

    @pl.when(t == 0)
    def _():
        loop(0, L, lambda d: pin.__setitem__(d, jnp.zeros(pin.shape[1:], BF16)))

    @pl.when(t == T - 1)
    def _():
        loop(0, L, lambda d: qin.__setitem__(d, jnp.zeros(qin.shape[1:], BF16)))

    def c_hop(h):
        @pl.when(t - h >= 0)
        def _():
            c_copy(cols, t - h, 0, 0).wait_recv()
            pl.when(has_right)(lambda: c_copy(c_rows(t - h), t - h, h, 0).start())

        @pl.when(t + h < T)
        def _():
            c_copy(cols, t + h, 0, 1).wait_recv()
            pl.when(has_left)(lambda: c_copy(c_rows(t + h), t + h, h, 1).start())

    def p_copy(src, d):
        return remote(src, pin.at[d], ps.at[d], pr.at[d], "tensor", right)

    def q_copy(src, d):
        return remote(src, qin.at[d], qs.at[d], qr.at[d], "tensor", lft)

    def s_step(k):
        d = k - t

        @pl.when((d >= 0) & (d < L))
        def _():
            @pl.when(t == 0)
            def _():
                p_copy(own.at[d], d).start()

            @pl.when(has_left)
            def _():
                p_copy(own.at[d], d).wait_recv()

                @pl.when(has_right)
                def _():
                    pout[d] = (pin[d].astype(F32) + own[d].astype(F32)).astype(BF16)
                    p_copy(pout.at[d], d).start()

        e = k - (T - 1 - t)

        @pl.when((e >= 0) & (e < L))
        def _():
            @pl.when(t == T - 1)
            def _():
                q_copy(own.at[e], e).start()

            @pl.when(has_right)
            def _():
                q_copy(own.at[e], e).wait_recv()

                @pl.when(has_left)
                def _():
                    qout[e] = (qin[e].astype(F32) + own[e].astype(F32)).astype(BF16)
                    q_copy(qout.at[e], e).start()

    half = L // 2

    def arrive(d):
        j = lax.rem(me - d + L, L)
        pl.when(d > 0)(lambda: g_copy(j, j).wait_recv())
        block = gg[j]
        own[d] = dot(rows_basis_t[...], block).astype(BF16)
        wide = block.astype(F32)
        gacc[...] += jnp.sum(wide * wide, axis=0, keepdims=True)
        for h in range(1, T - 1):
            pl.when(d == (h * L) // (T - 1))(lambda h=h: c_hop(h))
        pl.when(d < half)(lambda: s_step(d))

    loop(0, L, arrive)
    c_hop(T - 1)

    def mid_step(j):
        mid[...] += dot(gg[j], call[pl.ds(pl.multiple_of(j * W, W), W), :])

    loop(0, L, mid_step)
    core_out[...] = dot(rows_basis_t[...], mid[...].astype(BF16)).astype(BF16)

    def k_copy(slot, dst):
        return remote(core_out, core_in.at[slot], ks.at[dst], kr.at[slot], "tensor", dst)

    loop(1, T, lambda d: k_copy(t, lax.rem(t + d, T)).start())
    core_in[t] = core_out[...]
    s_step(half)
    for d in range(1, T):
        s = lax.rem(t + d, T)
        k_copy(s, s).wait_recv()
    core = core_in[0].astype(F32)
    for s in range(1, T):
        core = core + core_in[s].astype(F32)
    core = (core * dr[:, :1]).astype(BF16)
    mixed = base[0:1, 0:1] * mid[...] + dot(rows_basis[...], core)
    left[...] = (mixed * dc[0:1, :]).astype(BF16)

    def o_copy(slot, dst):
        return remote(raw_out.at[dst], raw_in.at[slot], os_.at[dst], or_.at[slot], "layer", dst)

    def emit(d):
        j = lax.rem(me - d + L, L)
        total = own[d].astype(F32) + pin[d].astype(F32) + qin[d].astype(F32)
        scaled = (total * dr[:, :1]).astype(BF16)
        raw = base[2:3, 0:1] * gg[j].astype(F32)
        raw = raw + base[1:2, 0:1] * dot(rows_basis[...], scaled)
        raw = raw + lax.dot_general(
            left[...], call[pl.ds(pl.multiple_of(j * W, W), W), :],
            (((1,), (1,)), ((), ())), preferred_element_type=F32)
        uacc[...] += jnp.sum(raw * raw, axis=0, keepdims=True)

        @pl.when(d == 0)
        def _():
            raw_in[me] = raw.astype(BF16)

        @pl.when(d > 0)
        def _():
            raw_out[j] = raw.astype(BF16)
            o_copy(me, j).start()

    last = T - 1

    def tail_step(k):
        pl.when(k > half)(lambda: s_step(k))
        pl.when(k - last >= 0)(lambda: emit(k - last))

    loop(min(last, half + 1), L + last, tail_step)

    nsend[0:8, :] = jnp.broadcast_to(jnp.sum(gacc[...]), (8, 128))
    nsend[8:16, :] = jnp.broadcast_to(jnp.sum(uacc[...]), (8, 128))

    def n_copy(slot, dst):
        return remote(nsend, nrecv.at[slot], ns.at[dst], nr.at[slot], "tensor", dst)

    loop(1, T, lambda d: n_copy(t, lax.rem(t + d, T)).start())
    nrecv[t] = nsend[...]
    for d in range(1, T):
        s = lax.rem(t + d, T)
        n_copy(s, s).wait_recv()
    sq = nrecv[0]
    for s in range(1, T):
        sq = sq + nrecv[s]
    fsend[...] = jnp.sqrt((sq[0:8] + 1.0) / (sq[8:16] + 1.0))

    def f_copy(slot, dst):
        return remote(fsend, frecv.at[slot], fs.at[dst], fr.at[slot], "layer", dst)

    loop(1, L, lambda d: f_copy(me, lax.rem(me + d, L)).start())
    frecv[me] = fsend[...]

    def finish(d):
        j = lax.rem(me + d, L)

        @pl.when(d > 0)
        def _():
            o_copy(j, j).wait_recv()
            f_copy(j, j).wait_recv()

        out[j] = (raw_in[j].astype(F32) * frecv[j][0:1, 0:1]).astype(BF16)

    loop(0, L, finish)

    def drain_layer(d):
        j = lax.rem(me + d, L)
        g_copy(me, j).wait_send()
        o_copy(me, j).wait_send()
        f_copy(me, j).wait_send()

    loop(1, L, drain_layer)

    def drain_tensor(d):
        s = lax.rem(t + d, T)
        k_copy(t, s).wait_send()
        n_copy(t, s).wait_send()

    loop(1, T, drain_tensor)

    def drain_line(d):
        pl.when(has_right)(lambda: p_copy(own.at[d], d).wait_send())
        pl.when(has_left)(lambda: q_copy(own.at[d], d).wait_send())

    loop(0, L, drain_line)
    for h in range(T - 1):
        pl.when((t - h >= 0) & has_right)(lambda h=h: c_copy(cols, t, h, 0).wait_send())
        pl.when((t + h < T) & has_left)(lambda h=h: c_copy(cols, t, h, 1).wait_send())


def solution(mesh):
    L, T = mesh.shape["layer"], mesh.shape["tensor"]

    def body(gradient, row_basis, column_basis, row_eigen, column_eigen, row_escape, column_escape):
        row_base = row_escape ** (-0.25)
        column_base = column_escape ** (-0.25)
        row_coef = (row_eigen + row_escape[:, None]) ** (-0.25) - row_base[:, None]
        column_coef = (column_eigen + column_escape[:, None]) ** (-0.25) - column_base[:, None]
        _, r, W = gradient.shape
        _, Cr, K = column_basis.shape
        dr = jnp.broadcast_to(row_coef[0][:, None], (K, 128))
        dc = jnp.broadcast_to(column_coef, (8, K))
        base = jnp.broadcast_to(
            jnp.concatenate([row_base, column_base, row_base * column_base] + [row_base] * 5)[:, None], (8, 128))
        vmem = pl.BlockSpec(memory_space=pltpu.VMEM)
        chunk = pltpu.VMEM((L, K, W), BF16)
        block = pltpu.VMEM((L, r, W), BF16)
        sem = pltpu.SemaphoreType.DMA
        return pl.pallas_call(
            functools.partial(kernel, L, T),
            out_shape=jax.ShapeDtypeStruct((L, r, W), BF16),
            in_specs=[vmem] * 7,
            out_specs=vmem,
            scratch_shapes=[
                block, chunk, chunk, chunk, chunk, chunk,
                pltpu.VMEM((T * Cr, K), BF16),
                pltpu.VMEM((r, K), F32),
                pltpu.VMEM((r, K), BF16),
                pltpu.VMEM((K, K), BF16),
                pltpu.VMEM((T, K, K), BF16),
                block, block,
                pltpu.VMEM((1, W), F32),
                pltpu.VMEM((1, W), F32),
                pltpu.VMEM((16, 128), F32),
                pltpu.VMEM((T, 16, 128), F32),
                pltpu.VMEM((8, 128), F32),
                pltpu.VMEM((L, 8, 128), F32),
                sem((L,)), sem((L,)),
                sem((2, T)), sem((T,)),
                sem((L,)), sem((L,)),
                sem((L,)), sem((L,)),
                sem((T,)), sem((T,)),
                sem((L,)), sem((L,)),
                sem((T,)), sem((T,)),
                sem((L,)), sem((L,)),
            ],
            compiler_params=pltpu.CompilerParams(
                collective_id=0, has_side_effects=True, vmem_limit_bytes=62 * 1024 * 1024),
        )(gradient, row_basis[0], row_basis[0].T, column_basis[0], dr, dc, base)

    in_specs = (
        P(None, "tensor", "layer"),
        P("layer", "tensor", None),
        P("layer", "tensor", None),
        P("layer", None),
        P("layer", None),
        P("layer"),
        P("layer"),
    )
    out_specs = P(None, "tensor", "layer")
    return jax.shard_map(body, mesh=mesh, in_specs=in_specs, out_specs=out_specs, check_vma=False)
```

time: 559 us -> 228 us (0.41)
  waiting for transfers between devices: 253 us -> 0 us
  Pallas kernels: 0 us -> 216 us
  blocking collectives: 119 us -> 0 us
  local copies, waits for them, and re-layouts: 84.7 us -> 8.39 us
  other arithmetic: 54.9 us -> 1.39 us
  matrix products: 30.3 us -> 0 us
  between operations: 15.9 us -> 1.42 us
    pallas_call x0 -> x1, Pallas kernels: none -> 216 us  [body(): pl.pallas_call(functools.partial(kernel, L, T), out_shape=jax.ShapeDtypeS...]
    all_gather x2 -> x0, waiting for transfers between devices: 150 us -> none  [the longest x1 75 us: body(): lax.all_gather(scaled, 'tensor', axis=0, tiled=True)]
    all_to_all x2 -> x0, blocking collectives: 108 us -> none  [the longest x1 54.5 us: body(): lax.all_to_all(gradient, 'layer', split_axis=0, concat_axis=2, tiled=True)]
    reduce_scatter x1 -> x0, waiting for transfers between devices: 75.4 us -> none  [body(): lax.psum_scatter(jnp.einsum('lrk,lrd->dlk', row_basis, group_block, prefe...]
    convert_element_type x1 -> x0, local copies, waits for them, and re-layouts: 49.5 us -> none  [finish(): return (raw_update * factor[:, None, None]).astype(jnp.bfloat16)]
    unnamed x1 -> x0, other arithmetic: 43.5 us -> none
    dot_general x5 -> x0, matrix products: 30.3 us -> none  [the longest x1 11 us: body(): jnp.einsum('lrk,ldk->lrd', left_factor, whole_columns, preferred_element_...]
    psum x1 -> x0, waiting for transfers between devices: 27.3 us -> none  [body(): core_mat = lax.psum(core_part.astype(jnp.bfloat16), 'tensor')]
  transfers between devices with their start and end apart: 4 -> 0, of which waited for: 4 -> 0; matrix products, arithmetic and copies ran while one was open for 4% -> 0% of each run, Pallas kernels for 0% -> 0%
where the time goes in v1:
time: 228 us; the launch traced here: 227 us
  Pallas kernels  216 us (95%)
  local copies, waits for them, and re-layouts  8.39 us (4%)
    pallas_call x1, Pallas kernels, body(): pl.pallas_call(functools.partial(kernel, L, T), out_shape=jax.ShapeDtypeS...  216 us
    unnamed x2, local copies, waits for them, and re-layouts  6.3 us

profile of v1, /device:TPU:0, one launch (start us, length us, event | category | flops | bytes accessed | tf_op | source)
XLA Modules:
  0.0 226.8 jit_solution(11734704911617709925)
XLA Ops:
  1.4 0.1 concatenate.3
  1.5 0.7 power_subtract_fusion
  2.2 0.7 power_subtract_fusion.1
  2.9 0.7 broadcast_in_dim.28.base
  3.5 0.6 broadcast_in_dim.13.dc
  4.1 0.7 broadcast_in_dim.11.dr
  4.9 1.7 copy.8
  6.5 215.6 %shard_map.73 = bf16[8,256,1024]{2,1,0:T(8,128)(2,1)} custom-call(bf16[8,256,1024]{2,1,0:T(8,128)(2,1)} %g.1, bf16[256,256]{1,0:T(8,128)(2,1)} %bitcast.14, bf16[256,256]{1,0:T(8,128)(2,1)} %bitcast.15, bf16[2048,256]{1,0:T(8,128)(2,1)} %bitcast.13, f32[256,128]{1,0:T(8,128)} %broadcast_in_dim.11.dr, f32[8,256]{1,0:T(8,128)} %broadcast_in_dim.13.dc, ...), custom_call_target="tpu_custom_call" | custom-call | tf_op jit(solution)/shard_map/pallas_call | solution.py:284
  222.2 4.6 %copy.14 = bf16[8,256,1024]{2,1,0:T(8,128)(2,1)} copy(bf16[8,256,1024]{2,1,0:T(8,128)(2,1)} %shard_map.73) | data formatting | bytes 8388608

commit v2 on v1

--- a/solution.py
+++ b/solution.py
@@ -38,8 +38,8 @@
 def kernel(
     L, T,
     g, rows_basis, rows_basis_t, cols, dr, dc, base,
-    out,
-    gg, own, pin, qin, pout, qout, call, mid, left, core_out, core_in, raw_out, raw_in,
+    out, factor,
+    gg, own, pin, qin, pout, qout, call, mid, left, core_out, core_in, core_sum, raw_out,
     gacc, uacc, nsend, nrecv, fsend, frecv,
     gs, gr, cs, cr, ps, pr, qs, qr, ks, kr, os_, or_, ns, nr, fs, fr,
 ):
@@ -100,53 +100,47 @@
     def q_copy(src, d):
         return remote(src, qin.at[d], qs.at[d], qr.at[d], "tensor", lft)
 
-    def s_step(k):
+    def end_send(d):
+        pl.when(t == 0)(lambda: p_copy(own.at[d], d).start())
+        pl.when(t == T - 1)(lambda: q_copy(own.at[d], d).start())
+
+    def forward(k):
         d = k - t
 
-        @pl.when((d >= 0) & (d < L))
-        def _():
-            @pl.when(t == 0)
+        @pl.when((d >= 0) & (d < L) & has_left)
+        def _():
+            p_copy(own.at[d], d).wait_recv()
+
+            @pl.when(has_right)
             def _():
-                p_copy(own.at[d], d).start()
+                pout[d] = (pin[d].astype(F32) + own[d].astype(F32)).astype(BF16)
+                p_copy(pout.at[d], d).start()
+
+        e = k - (T - 1 - t)
+
+        @pl.when((e >= 0) & (e < L) & has_right)
+        def _():
+            q_copy(own.at[e], e).wait_recv()
 
             @pl.when(has_left)
             def _():
-                p_copy(own.at[d], d).wait_recv()
-
-                @pl.when(has_right)
-                def _():
-                    pout[d] = (pin[d].astype(F32) + own[d].astype(F32)).astype(BF16)
-                    p_copy(pout.at[d], d).start()
-
-        e = k - (T - 1 - t)
-
-        @pl.when((e >= 0) & (e < L))
-        def _():
-            @pl.when(t == T - 1)
-            def _():
-                q_copy(own.at[e], e).start()
-
-            @pl.when(has_right)
-            def _():
-                q_copy(own.at[e], e).wait_recv()
-
-                @pl.when(has_left)
-                def _():
-                    qout[e] = (qin[e].astype(F32) + own[e].astype(F32)).astype(BF16)
-                    q_copy(qout.at[e], e).start()
+                qout[e] = (qin[e].astype(F32) + own[e].astype(F32)).astype(BF16)
+                q_copy(qout.at[e], e).start()
 
     half = L // 2
+    early = ((T - 2) * L) // (T - 1) + 1
 
     def arrive(d):
         j = lax.rem(me - d + L, L)
         pl.when(d > 0)(lambda: g_copy(j, j).wait_recv())
         block = gg[j]
         own[d] = dot(rows_basis_t[...], block).astype(BF16)
+        pl.when(d < half)(lambda: end_send(d))
         wide = block.astype(F32)
         gacc[...] += jnp.sum(wide * wide, axis=0, keepdims=True)
         for h in range(1, T - 1):
             pl.when(d == (h * L) // (T - 1))(lambda h=h: c_hop(h))
-        pl.when(d < half)(lambda: s_step(d))
+        pl.when(d >= early)(lambda: forward(d - early + 1))
 
     loop(0, L, arrive)
     c_hop(T - 1)
@@ -157,24 +151,54 @@
     loop(0, L, mid_step)
     core_out[...] = dot(rows_basis_t[...], mid[...].astype(BF16)).astype(BF16)
 
-    def k_copy(slot, dst):
-        return remote(core_out, core_in.at[slot], ks.at[dst], kr.at[slot], "tensor", dst)
-
-    loop(1, T, lambda d: k_copy(t, lax.rem(t + d, T)).start())
-    core_in[t] = core_out[...]
-    s_step(half)
-    for d in range(1, T):
-        s = lax.rem(t + d, T)
-        k_copy(s, s).wait_recv()
-    core = core_in[0].astype(F32)
-    for s in range(1, T):
-        core = core + core_in[s].astype(F32)
-    core = (core * dr[:, :1]).astype(BF16)
-    mixed = base[0:1, 0:1] * mid[...] + dot(rows_basis[...], core)
-    left[...] = (mixed * dc[0:1, :]).astype(BF16)
+    def kp_copy(src):
+        return remote(src, core_in.at[0], ks.at[0], kr.at[0], "tensor", right)
+
+    def kq_copy(src):
+        return remote(src, core_in.at[1], ks.at[1], kr.at[1], "tensor", lft)
+
+    @pl.when(t == 0)
+    def _():
+        core_in[0] = jnp.zeros(core_out.shape, BF16)
+        kp_copy(core_out).start()
+
+    @pl.when(t == T - 1)
+    def _():
+        core_in[1] = jnp.zeros(core_out.shape, BF16)
+        kq_copy(core_out).start()
+
+    loop(half, L, end_send)
+
+    def core_step(k):
+        @pl.when((k == half + t) & has_left)
+        def _():
+            kp_copy(core_out).wait_recv()
+
+            @pl.when(has_right)
+            def _():
+                core_sum[0] = (core_in[0].astype(F32) + core_out[...].astype(F32)).astype(BF16)
+                kp_copy(core_sum.at[0]).start()
+
+        @pl.when((k == half + T - 1 - t) & has_right)
+        def _():
+            kq_copy(core_out).wait_recv()
+
+            @pl.when(has_left)
+            def _():
+                core_sum[1] = (core_in[1].astype(F32) + core_out[...].astype(F32)).astype(BF16)
+                kq_copy(core_sum.at[1]).start()
+
+    def make_left():
+        core = core_in[0].astype(F32) + core_in[1].astype(F32) + core_out[...].astype(F32)
+        core = (core * dr[:, :1]).astype(BF16)
+        mixed = base[0:1, 0:1] * mid[...] + dot(rows_basis[...], core)
+        left[...] = (mixed * dc[0:1, :]).astype(BF16)
 
     def o_copy(slot, dst):
-        return remote(raw_out.at[dst], raw_in.at[slot], os_.at[dst], or_.at[slot], "layer", dst)
+        return remote(raw_out.at[dst], out.at[slot], os_.at[dst], or_.at[slot], "layer", dst)
+
+    def own_copy():
+        return pltpu.make_async_copy(raw_out.at[me], out.at[me], os_.at[me])
 
     def emit(d):
         j = lax.rem(me - d + L, L)
@@ -185,24 +209,24 @@
         raw = raw + lax.dot_general(
             left[...], call[pl.ds(pl.multiple_of(j * W, W), W), :],
             (((1,), (1,)), ((), ())), preferred_element_type=F32)
+        raw_out[j] = raw.astype(BF16)
+        pl.when(d == 0)(lambda: own_copy().start())
+        pl.when(d > 0)(lambda: o_copy(me, j).start())
         uacc[...] += jnp.sum(raw * raw, axis=0, keepdims=True)
 
-        @pl.when(d == 0)
-        def _():
-            raw_in[me] = raw.astype(BF16)
-
-        @pl.when(d > 0)
-        def _():
-            raw_out[j] = raw.astype(BF16)
-            o_copy(me, j).start()
-
-    last = T - 1
+    first = half + T - 1
+
+    def upto(k):
+        return jnp.minimum(k - T + 2, 3 + 2 * (k - first))
 
     def tail_step(k):
-        pl.when(k > half)(lambda: s_step(k))
-        pl.when(k - last >= 0)(lambda: emit(k - last))
-
-    loop(min(last, half + 1), L + last, tail_step)
+        core_step(k)
+        forward(k)
+        pl.when(k == first)(make_left)
+        pl.when(k == first)(lambda: loop(0, upto(k), emit))
+        pl.when(k > first)(lambda: loop(upto(k - 1), upto(k), emit))
+
+    loop(L - early + 1, L + T - 1, tail_step)
 
     nsend[0:8, :] = jnp.broadcast_to(jnp.sum(gacc[...]), (8, 128))
     nsend[8:16, :] = jnp.broadcast_to(jnp.sum(uacc[...]), (8, 128))
@@ -225,18 +249,15 @@
 
     loop(1, L, lambda d: f_copy(me, lax.rem(me + d, L)).start())
     frecv[me] = fsend[...]
+    own_copy().wait()
 
     def finish(d):
         j = lax.rem(me + d, L)
-
-        @pl.when(d > 0)
-        def _():
-            o_copy(j, j).wait_recv()
-            f_copy(j, j).wait_recv()
-
-        out[j] = (raw_in[j].astype(F32) * frecv[j][0:1, 0:1]).astype(BF16)
-
-    loop(0, L, finish)
+        o_copy(j, j).wait_recv()
+        f_copy(j, j).wait_recv()
+
+    loop(1, L, finish)
+    factor[...] = frecv[...]
 
     def drain_layer(d):
         j = lax.rem(me + d, L)
@@ -245,10 +266,11 @@
         f_copy(me, j).wait_send()
 
     loop(1, L, drain_layer)
+    pl.when(has_right)(lambda: kp_copy(core_out).wait_send())
+    pl.when(has_left)(lambda: kq_copy(core_out).wait_send())
 
     def drain_tensor(d):
         s = lax.rem(t + d, T)
-        k_copy(t, s).wait_send()
         n_copy(t, s).wait_send()
 
     loop(1, T, drain_tensor)
@@ -281,19 +303,20 @@
         chunk = pltpu.VMEM((L, K, W), BF16)
         block = pltpu.VMEM((L, r, W), BF16)
         sem = pltpu.SemaphoreType.DMA
-        return pl.pallas_call(
+        raw, factor = pl.pallas_call(
             functools.partial(kernel, L, T),
-            out_shape=jax.ShapeDtypeStruct((L, r, W), BF16),
+            out_shape=(jax.ShapeDtypeStruct((L, r, W), BF16), jax.ShapeDtypeStruct((L, 8, 128), F32)),
             in_specs=[vmem] * 7,
-            out_specs=vmem,
+            out_specs=(pl.BlockSpec(memory_space=pl.ANY), vmem),
             scratch_shapes=[
                 block, chunk, chunk, chunk, chunk, chunk,
                 pltpu.VMEM((T * Cr, K), BF16),
                 pltpu.VMEM((r, K), F32),
                 pltpu.VMEM((r, K), BF16),
                 pltpu.VMEM((K, K), BF16),
-                pltpu.VMEM((T, K, K), BF16),
-                block, block,
+                pltpu.VMEM((2, K, K), BF16),
+                pltpu.VMEM((2, K, K), BF16),
+                block,
                 pltpu.VMEM((1, W), F32),
                 pltpu.VMEM((1, W), F32),
                 pltpu.VMEM((16, 128), F32),
@@ -304,7 +327,7 @@
                 sem((2, T)), sem((T,)),
                 sem((L,)), sem((L,)),
                 sem((L,)), sem((L,)),
-                sem((T,)), sem((T,)),
+                sem((2,)), sem((2,)),
                 sem((L,)), sem((L,)),
                 sem((T,)), sem((T,)),
                 sem((L,)), sem((L,)),
@@ -312,6 +335,7 @@
             compiler_params=pltpu.CompilerParams(
                 collective_id=0, has_side_effects=True, vmem_limit_bytes=62 * 1024 * 1024),
         )(gradient, row_basis[0], row_basis[0].T, column_basis[0], dr, dc, base)
+        return (raw.astype(F32) * factor[:, :1, :1]).astype(BF16)
 
     in_specs = (
         P(None, "tensor", "layer"),

time: 228 us -> 211 us (0.925)
  Pallas kernels: 216 us -> 197 us
  other arithmetic: 1.39 us -> 7.37 us
  local copies, waits for them, and re-layouts: 8.39 us -> 4.65 us
    pallas_call x1, Pallas kernels: 216 us -> 197 us  [body(): pl.pallas_call(functools.partial(kernel, L, T), out_shape=(jax.ShapeDtype...]
    convert_element_type x0 -> x1, other arithmetic: none -> 5.97 us  [body(): return (raw.astype(F32) * factor[:, :1, :1]).astype(BF16)]
    unnamed x2 -> x1, local copies, waits for them, and re-layouts: 6.3 us -> 1.66 us
where the time goes in v2:
time: 211 us; the launch traced here: 210 us
  Pallas kernels  197 us (93%)
  other arithmetic  7.37 us (3%)
  local copies, waits for them, and re-layouts  4.65 us (2%)
    pallas_call x1, Pallas kernels, body(): pl.pallas_call(functools.partial(kernel, L, T), out_shape=(jax.ShapeDtype...  197 us
    convert_element_type x1, other arithmetic, body(): return (raw.astype(F32) * factor[:, :1, :1]).astype(BF16)  5.97 us

profile of v2, /device:TPU:0, one launch (start us, length us, event | category | flops | bytes accessed | tf_op | source)
XLA Modules:
  0.0 210.4 jit_solution(13482821854144393164)
XLA Ops:
  1.4 0.1 concatenate.3
  1.5 0.7 power_subtract_fusion
  2.2 0.7 power_subtract_fusion.1
  2.9 0.7 broadcast_in_dim.28.base
  3.5 0.6 broadcast_in_dim.13.dc
  4.1 0.7 broadcast_in_dim.11.dr
  4.9 1.7 copy.10
  6.5 197.0 %shard_map.73 = (bf16[8,256,1024]{2,1,0:T(8,128)(2,1)}, f32[8,8,128]{2,1,0:T(8,128)}) custom-call(bf16[8,256,1024]{2,1,0:T(8,128)(2,1)} %g.1, bf16[256,256]{1,0:T(8,128)(2,1)} %bitcast.14, bf16[256,256]{1,0:T(8,128)(2,1)} %bitcast.15, bf16[2048,256]{1,0:T(8,128)(2,1)} %bitcast.13, f32[256,128]{1,0:T(8,128)} %broadcast_in_dim.11.dr, ...), custom_call_target="tpu_custom_call" | custom-call | tf_op jit(solution)/shard_map/pallas_call | solution.py:306
  203.5 0.9 slice_reduce_fusion
  204.4 6.0 %multiply_convert_fusion = bf16[8,256,1024]{2,1,0:T(8,128)(2,1)} fusion(bf16[8,256,1024]{2,1,0:T(8,128)(2,1)} %get-tuple-element.7, f32[8]{0:T(128)S(1)} %slice_reduce_fusion), kind=kLoop, calls=%fused_computation | loop fusion | flops 6291456 | bytes 8388640 | tf_op jit(solution)/shard_map/convert_element_type | solution.py:338

commit v3 on v2

--- a/solution.py
+++ b/solution.py
@@ -131,11 +131,11 @@
     early = ((T - 2) * L) // (T - 1) + 1
 
     def arrive(d):
-        j = lax.rem(me - d + L, L)
-        pl.when(d > 0)(lambda: g_copy(j, j).wait_recv())
+        j = lax.rem(me - 1 - d + L, L)
+        pl.when(d < L - 1)(lambda: g_copy(j, j).wait_recv())
         block = gg[j]
         own[d] = dot(rows_basis_t[...], block).astype(BF16)
-        pl.when(d < half)(lambda: end_send(d))
+        pl.when(d <= half)(lambda: end_send(d))
         wide = block.astype(F32)
         gacc[...] += jnp.sum(wide * wide, axis=0, keepdims=True)
         for h in range(1, T - 1):
@@ -167,7 +167,7 @@
         core_in[1] = jnp.zeros(core_out.shape, BF16)
         kq_copy(core_out).start()
 
-    loop(half, L, end_send)
+    loop(half + 1, L, end_send)
 
     def core_step(k):
         @pl.when((k == half + t) & has_left)
@@ -201,7 +201,7 @@
         return pltpu.make_async_copy(raw_out.at[me], out.at[me], os_.at[me])
 
     def emit(d):
-        j = lax.rem(me - d + L, L)
+        j = lax.rem(me - 1 - d + L, L)
         total = own[d].astype(F32) + pin[d].astype(F32) + qin[d].astype(F32)
         scaled = (total * dr[:, :1]).astype(BF16)
         raw = base[2:3, 0:1] * gg[j].astype(F32)
@@ -210,14 +210,15 @@
             left[...], call[pl.ds(pl.multiple_of(j * W, W), W), :],
             (((1,), (1,)), ((), ())), preferred_element_type=F32)
         raw_out[j] = raw.astype(BF16)
-        pl.when(d == 0)(lambda: own_copy().start())
-        pl.when(d > 0)(lambda: o_copy(me, j).start())
+        pl.when(d == L - 1)(lambda: own_copy().start())
+        pl.when(d < L - 1)(lambda: o_copy(me, j).start())
         uacc[...] += jnp.sum(raw * raw, axis=0, keepdims=True)
 
     first = half + T - 1
 
     def upto(k):
-        return jnp.minimum(k - T + 2, 3 + 2 * (k - first))
+        paced = jnp.minimum(k - T + 2, 3 + 2 * (k - first))
+        return jnp.where(has_left & has_right, paced, k - T + 2)
 
     def tail_step(k):
         core_step(k)

time: 211 us -> 204 us (0.967)
  Pallas kernels: 197 us -> 190 us
    pallas_call x1, Pallas kernels: 197 us -> 190 us  [body(): pl.pallas_call(functools.partial(kernel, L, T), out_shape=(jax.ShapeDtype...]
where the time goes in v3:
time: 204 us
  Pallas kernels  190 us (93%)
  other arithmetic  7.37 us (4%)
  local copies, waits for them, and re-layouts  4.65 us (2%)
    pallas_call x1, Pallas kernels, body(): pl.pallas_call(functools.partial(kernel, L, T), out_shape=(jax.ShapeDtype...  190 us
    convert_element_type x1, other arithmetic, body(): return (raw.astype(F32) * factor[:, :1, :1]).astype(BF16)  5.97 us

profile of v3, /device:TPU:0, one launch (start us, length us, event | category | flops | bytes accessed | tf_op | source)
XLA Modules:
  0.0 203.8 jit_solution(12756830800866886340)
XLA Ops:
  1.4 0.1 concatenate.3
  1.5 0.7 power_subtract_fusion
  2.2 0.7 power_subtract_fusion.1
  2.9 0.7 broadcast_in_dim.28.base
  3.5 0.6 broadcast_in_dim.13.dc
  4.1 0.7 broadcast_in_dim.11.dr
  4.9 1.7 copy.10
  6.5 190.4 %shard_map.73 = (bf16[8,256,1024]{2,1,0:T(8,128)(2,1)}, f32[8,8,128]{2,1,0:T(8,128)}) custom-call(bf16[8,256,1024]{2,1,0:T(8,128)(2,1)} %g.1, bf16[256,256]{1,0:T(8,128)(2,1)} %bitcast.14, bf16[256,256]{1,0:T(8,128)(2,1)} %bitcast.15, bf16[2048,256]{1,0:T(8,128)(2,1)} %bitcast.13, f32[256,128]{1,0:T(8,128)} %broadcast_in_dim.11.dr, ...), custom_call_target="tpu_custom_call" | custom-call | tf_op jit(solution)/shard_map/pallas_call | solution.py:307
  196.9 0.9 slice_reduce_fusion
  197.8 6.0 %multiply_convert_fusion = bf16[8,256,1024]{2,1,0:T(8,128)(2,1)} fusion(bf16[8,256,1024]{2,1,0:T(8,128)(2,1)} %get-tuple-element.7, f32[8]{0:T(128)S(1)} %slice_reduce_fusion), kind=kLoop, calls=%fused_computation | loop fusion | flops 6291456 | bytes 8388640 | tf_op jit(solution)/shard_map/convert_element_type | solution.py:339
